TPU v7x, 32 devices: a whole 2x2x4 slice. The times are simulated.
32 devices in a mesh: row: 2 (over core), col: 16 (over z, y, x).
Axes of the slice: x: 2, y: 2, z: 4, core: 2. Of those that a mesh axis runs over, the one named last changes fastest.
Arguments:
- object_in: float32 [2, 2, 512, 4096], P(None, None, 'row', 'col'), may hold values from -4 to 4
- probe_in: float32 [2, 256, 256], replicated, may hold values from -5 to 5
- positions: int32 [2, 16, 2, 2], P('row', 'col'), may hold values from -32 to 32
- intensity: float32 [2, 16, 2, 256, 256], P('row', 'col'), may hold values from 0.1 to 8.2
Outputs:
- object_out: float32 [2, 2, 512, 4096], P(None, None, 'row', 'col')
- probe_out: float32 [2, 256, 256], replicated
Inputs may be any that keep to these rules, and one draw needn't show every extreme that they name: positions[r, c, p] = (dy, dx) places the probe of position p on object rows r * 256 + dy to r * 256 + dy + 255 and columns c * 256 + dx to c * 256 + dx + 255.
All inputs are finite; a program needn't handle non-finite values.
Results may differ from a plain program's by a relative error of at most 0.0003.
Values sent between devices are 32-bit elements; how exact they have to be, the bound alone decides.
No kernel may reach another device: no remote copies, remote signals or barrier semaphores. Data moves between devices by JAX's collectives and lax.ppermute only.
A program may use at most 64 MiB of HBM per device.

v0:
```python
import math
import jax
import jax.numpy as jnp
from jax import lax
from jax.sharding import PartitionSpec as P

RIM = 32


def passed_along(value, axis, steps):
    count = lax.axis_size(axis)
    initial, last = (max(0, -steps), min(count, count - steps))
    return lax.ppermute(value, axis, [(source, source + steps) for source in range(initial, last)])


def extended(cells, sides, width):
    for axis, dim in sides:
        count = lax.axis_size(axis)
        ends = count - 1
        head = lax.slice_in_dim(cells, 0, width, axis=dim)
        tail = lax.slice_in_dim(cells, cells.shape[dim] - width, cells.shape[dim], axis=dim)
        cells = jnp.concatenate(
            [
                lax.ppermute(tail, axis, [(i, (i + 1) % count) for i in range(ends)]),
                cells,
                lax.ppermute(head, axis, [((i + 1) % count, i) for i in range(ends)]),
            ],
            axis=dim,
        )
    return cells


def tables(extent):
    line_idx = jnp.arange(extent, dtype=jnp.int32)
    turn_count = line_idx[:, None] * line_idx[None, :] % extent
    angles = turn_count.astype(jnp.float32) * (2.0 * math.pi / extent)
    factor = 1.0 / math.sqrt(extent)
    cosine = jnp.cos(angles) * factor
    sine_tab = jnp.sin(angles) * factor
    frequency = ((line_idx + extent // 2) % extent - extent // 2).astype(jnp.float32)
    phases = (
        -math.pi * 8.0 / (extent * extent) * (frequency[:, None] ** 2 + frequency[None, :] ** 2)
    )
    return (cosine, sine_tab, jnp.cos(phases), jnp.sin(phases))


def matrices(cosine, sine_tab, orient):
    return (cosine, sine_tab, float(orient))


def transform(real_part, imag_part, tables_pair):
    cosine, sine_tab, orient = tables_pair
    high = lax.Precision.HIGHEST
    rc = jnp.einsum("byx,xk->byk", real_part, cosine, precision=high)
    rs = jnp.einsum("byx,xk->byk", real_part, sine_tab, precision=high)
    ic = jnp.einsum("byx,xk->byk", imag_part, cosine, precision=high)
    isn = jnp.einsum("byx,xk->byk", imag_part, sine_tab, precision=high)
    mid_re = rc + orient * isn
    mid_im = ic - orient * rs
    out_re = jnp.einsum("ky,byx->bkx", cosine, mid_re, precision=high) + orient * jnp.einsum(
        "ky,byx->bkx", sine_tab, mid_im, precision=high
    )
    out_im = jnp.einsum("ky,byx->bkx", cosine, mid_im, precision=high) - orient * jnp.einsum(
        "ky,byx->bkx", sine_tab, mid_re, precision=high
    )
    return (out_re, out_im)


def times_plain(first_re, first_im, second_re, second_im):
    return (
        first_re * second_re - first_im * second_im,
        first_re * second_im + first_im * second_re,
    )


def times_conj(first_re, first_im, second_re, second_im):
    return (
        first_re * second_re + first_im * second_im,
        first_re * second_im - first_im * second_re,
    )


def tile_gradient(window, probe, offsets, measured, constants):
    cosine, sine_tab, kern_re, kern_im = constants
    forward = matrices(cosine, sine_tab, 1)
    backward = matrices(cosine, sine_tab, -1)
    extent = probe.shape[-1]
    zero_idx = jnp.zeros((), jnp.int32)

    def cut_patch(offset):
        return lax.dynamic_slice(
            window, (zero_idx, zero_idx, offset[0] + RIM, offset[1] + RIM), (2, 2, extent, extent)
        )

    patches = jax.vmap(cut_patch)(offsets)
    first_re, first_im = (patches[:, 0, 0], patches[:, 0, 1])
    second_re, second_im = (patches[:, 1, 0], patches[:, 1, 1])
    probe_re, probe_im = (probe[0], probe[1])
    wave_re, wave_im = times_plain(probe_re, probe_im, first_re, first_im)
    spec_re, spec_im = transform(wave_re, wave_im, forward)
    spec_re, spec_im = times_plain(kern_re, kern_im, spec_re, spec_im)
    prop_re, prop_im = transform(spec_re, spec_im, backward)
    exit_re, exit_im = times_plain(prop_re, prop_im, second_re, second_im)
    far_re, far_im = transform(exit_re, exit_im, forward)
    excess = 2.0 * (far_re * far_re + far_im * far_im - measured)
    back_re, back_im = transform(excess * far_re, excess * far_im, backward)
    grad2_re, grad2_im = times_conj(prop_re, prop_im, back_re, back_im)
    lift_re, lift_im = times_conj(second_re, second_im, back_re, back_im)
    lift_re, lift_im = transform(lift_re, lift_im, forward)
    lift_re, lift_im = times_conj(kern_re, kern_im, lift_re, lift_im)
    enter_re, enter_im = transform(lift_re, lift_im, backward)
    grad1_re, grad1_im = times_conj(probe_re, probe_im, enter_re, enter_im)
    probe_re_g, probe_im_g = times_conj(first_re, first_im, enter_re, enter_im)
    probe_grad = jnp.stack([jnp.sum(probe_re_g, 0), jnp.sum(probe_im_g, 0)], 0)
    pieces = jnp.stack([jnp.stack([grad1_re, grad1_im], 1), jnp.stack([grad2_re, grad2_im], 1)], 1)
    gradient = jnp.zeros(window.shape, jnp.float32)
    for position in range(offsets.shape[0]):
        start_at = (zero_idx, zero_idx, offsets[position, 0] + RIM, offsets[position, 1] + RIM)
        current = lax.dynamic_slice(gradient, start_at, pieces.shape[1:])
        gradient = lax.dynamic_update_slice(gradient, current + pieces[position], start_at)
    return (gradient, probe_grad)


def turned(block):
    return jnp.swapaxes(block, 2, 3)


def rows_then_cols(gradient):
    inner_px = gradient.shape[-1] - 2 * RIM
    upper_end = RIM + inner_px
    from_below = passed_along(gradient[:, :, :RIM, :], "row", -1)
    from_above = passed_along(gradient[:, :, upper_end:, :], "row", 1)
    middle = gradient[:, :, RIM:upper_end, :]
    middle = middle.at[:, :, inner_px - RIM :, :].add(from_below)
    middle = middle.at[:, :, :RIM, :].add(from_above)
    from_right = turned(passed_along(turned(middle[..., :RIM]), "col", -1))
    from_left = turned(passed_along(turned(middle[..., upper_end:]), "col", 1))
    interior = middle[..., RIM:upper_end]
    interior = interior.at[..., inner_px - RIM :].add(from_right)
    interior = interior.at[..., :RIM].add(from_left)
    return interior


def local(object_in, probe_in, positions, intensity):
    extent = probe_in.shape[-1]
    constants = tables(extent)
    offsets = positions.reshape(-1, 2)
    measured = intensity.reshape(-1, extent, extent)
    tile_total = lax.axis_size("row") * lax.axis_size("col")
    probe_rate = 2.0 / tile_total
    current = object_in
    window = extended(current, (("row", 2), ("col", 3)), RIM)
    gradient, probe_grad = tile_gradient(window, probe_in, offsets, measured, constants)
    probe_total = lax.psum(probe_grad, ("row", "col"))
    probe_next = probe_in - probe_rate * probe_total
    descent = rows_then_cols(gradient)
    local_peak = jnp.max(descent[:, 0] ** 2 + descent[:, 1] ** 2)
    largest = lax.pmax(local_peak, ("row", "col"))
    current = current - 0.3 * descent / (jnp.sqrt(largest) + 1e-06)
    return (current, probe_next)


def solution(mesh):
    placed = (
        P(None, None, "row", "col"),
        P(),
        P("row", "col", None, None),
        P("row", "col", None, None, None),
    )
    return jax.shard_map(
        local,
        mesh=mesh,
        in_specs=placed,
        out_specs=(P(None, None, "row", "col"), P()),
        check_vma=False,
    )
```

profile of v0, /device:TPU:0, one launch (start us, length us, event | category | flops | bytes accessed | tf_op | source)
XLA Modules:
  0.0 372.2 jit_solution(18278796465916017940)
XLA Ops:
  10.1 2.4 collective-permute-start
  22.2 2.0 copy.98
  24.5 4.2 %collective-permute-start.2 = (f32[2,2,320,32]{2,3,1,0:T(8,128)S(1)}, f32[2,2,320,32]{2,3,1,0:T(8,128)S(1)}, u32[]{:S(2)}, u32[]{:S(2)}) collective-permute-start(f32[2,2,320,32]{2,3,1,0:T(8,128)S(1)} %get-tuple-element.84), channel_id=1, source_target_pairs={{0,1},{1,2},{2,3},{3,4},{4,5},{5,6},{6,7},{7,8},{8,9},{9,10},{10,1... | collective-permute-start | bytes 491528 | tf_op jit(solution)/shard_map/ppermute | solution.py:24
  30.1 3.7 collective-permute-done.2
  33.8 6.2 %collective-permute-done.3 = f32[2,2,320,32]{2,3,1,0:T(8,128)S(1)} collective-permute-done((f32[2,2,320,32]{2,3,1,0:T(8,128)S(1)}, f32[2,2,320,32]{2,3,1,0:T(8,128)S(1)}, u32[]{:S(2)}, u32[]{:S(2)}) %collective-permute-start.3) | collective-permute-done | bytes 163872 | tf_op jit(solution)/shard_map/ppermute | solution.py:26
  41.8 11.3 %while.5 = (s32[]{:T(128)}, f32[2,2,320,320]{2,3,1,0:T(8,128)S(1)}, s32[2,4]{1,0:T(2,128)S(1)}, f32[2,2,2,256,256]{3,4,0,2,1:T(8,128)}, s32[]{:T(128)}) while((s32[]{:T(128)}, f32[2,2,320,320]{2,3,1,0:T(8,128)S(1)}, s32[2,4]{1,0:T(2,128)S(1)}, f32[2,2,2,256,256]{3,4,0,2,1:T(8,128)}, s32[]{:T(128)}) %tuple.62), condition=%wide.while_cond.4, body=%wide.while_body.4.sunk | while | flops 2 | bytes 21496496 | solution.py:91
  53.1 3.4 fusion.112
  56.5 3.2 fusion.116
  67.2 2.3 fusion.22
  78.8 2.1 fusion.20
  84.6 1.9 fusion.32
  90.1 2.0 convolution_add_fusion.3
  101.4 1.9 fusion.92
  103.3 2.3 fusion.88
  105.7 1.9 fusion.13
  107.6 1.9 fusion.12
  115.1 2.2 add_bitcast_fusion
  126.4 2.1 fusion.82
  136.0 1.9 fusion.5
  137.9 2.3 fusion.4
  145.6 2.8 fusion.38
  150.1 13.4 %dynamic_update_slice.6 = f32[2,2,320,320]{2,3,1,0:T(8,128)S(1)} dynamic-update-slice(f32[2,2,320,320]{2,3,1,0:T(8,128)S(1)} %broadcast_in_dim.2, f32[2,2,256,256]{2,3,1,0:T(8,128)} %fusion.25, s32[]{:T(128)} %constant.162.clone.1, s32[]{:T(128)} %constant.162.clone.1, s32[]{:T(128)S(6)} %select_n.155, s32[]{:T(128)S(6)} %select_n.156) | dynamic-update-slice | bytes 2097156 | tf_op jit(solution)/shard_map/dynamic_update_slice | solution.py:120
  163.5 2.4 fusion.27
  165.9 14.0 %dynamic_update_slice.7 = f32[2,2,320,320]{2,3,1,0:T(8,128)S(1)} dynamic-update-slice(f32[2,2,320,320]{2,3,1,0:T(8,128)S(1)} %dynamic_update_slice.6, f32[2,2,256,256]{2,3,1,0:T(8,128)} %fusion.27, s32[]{:T(128)} %constant.162.clone.1, s32[]{:T(128)} %constant.162.clone.1, s32[]{:T(128)S(6)} %select_n.157, s32[]{:T(128)S(6)} %select_n.158) | dynamic-update-slice | bytes 2097156 | tf_op jit(solution)/shard_map/dynamic_update_slice | solution.py:120
  181.8 2.0 copy.129
  187.1 4.4 %collective-permute-start.5 = (f32[2,2,32,320]{3,2,1,0:T(8,128)}, f32[2,2,32,320]{3,2,1,0:T(8,128)}, u32[]{:S(2)}, u32[]{:S(2)}) collective-permute-start(f32[2,2,32,320]{3,2,1,0:T(8,128)} %copy.126), channel_id=1, source_target_pairs={{0,16},{1,17},{2,18},{3,19},{4,20},{5,21},{6,22},{7,23},{8,24},{9,... | collective-permute-start | bytes 491528 | tf_op jit(solution)/shard_map/ppermute | solution.py:13
  192.8 3.7 %scatter-add.14 = f32[2,2,256,320]{2,3,1,0:T(8,128)} dynamic-update-slice(f32[2,2,256,320]{2,3,1,0:T(8,128)} %slice.249, f32[2,2,32,320]{2,3,1,0:T(8,128)S(1)} %slice_add_fusion.1, s32[]{:T(128)} %constant.162.clone.1, s32[]{:T(128)} %constant.162.clone.1, s32[]{:T(128)} %constant.175.clone.1, s32[]{:T(128)} %constant.162.clone.1) | dynamic-update-slice | bytes 327684 | tf_op jit(solution)/shard_map/scatter-add | solution.py:134
  198.8 3.6 scatter-add.15
  206.8 4.7 %collective-permute-start.7 = (f32[2,2,32,256]{3,2,1,0:T(8,128)S(1)}, f32[2,2,32,256]{3,2,1,0:T(8,128)S(1)}, u32[]{:S(2)}, u32[]{:S(2)}) collective-permute-start(f32[2,2,32,256]{3,2,1,0:T(8,128)S(1)} %get-tuple-element.90), channel_id=1, source_target_pairs={{0,1},{1,2},{2,3},{3,4},{4,5},{5,6},{6,7},{7,8},{8,9},{9,10},{10,1... | collective-permute-start | bytes 393224 | tf_op jit(solution)/shard_map/ppermute | solution.py:13
  211.5 105.9 %all-reduce.2.cloned.1.call-done = f32[2,256,256]{1,2,0:T(8,128)} async-done(((f32[2,256,256]{1,2,0:T(8,128)}), f32[2,256,256]{1,2,0:T(8,128)}) %all-reduce.2.cloned.1.call-update) | async-done | bytes 524304 | tf_op jit(solution)/shard_map/psum | solution.py:154
  321.3 39.5 %pmax.7 = f32[]{:T(128)} all-reduce(f32[]{:T(128)} %fusion.29), channel_id=1, replica_groups=mesh['row'=2,'col'=16] {'row','col'}, use_global_device_ids=true, to_apply=%region_1.2 | all-reduce | flops 1 | bytes 8 | tf_op jit(solution)/shard_map/pmax | solution.py:158
  362.6 2.5 copy.130
  (129 shorter events, 102.3 us)
Async XLA Ops:
  7.2 6.7 %copy-start.15 = (s32[1,1,2,2]{3,2,1,0:T(2,128)S(1)}, s32[1,1,2,2]{3,2,1,0:T(2,128)}, u32[]{:S(2)}) copy-start(s32[1,1,2,2]{3,2,1,0:T(2,128)} %param.14) | copy-start | bytes 52
  7.2 12.2 %copy-start.12 = (f32[2,256,256]{2,1,0:T(8,128)S(1)}, f32[2,256,256]{2,1,0:T(8,128)}, u32[]{:S(2)}) copy-start(f32[2,256,256]{2,1,0:T(8,128)} %param.13) | copy-start | bytes 1572868
  7.2 310.2 %all-reduce.2.cloned.1.call-start = ((), (), s32[]{:S(2)}) async-start(), calls=%async_computation | async-start | bytes 1048576 | tf_op jit(solution)/shard_map/psum | solution.py:154
  8.8 31.1 %copy-start.2 = (f32[2,2,256,256]{2,3,1,0:T(8,128)}, f32[2,2,256,256]{2,3,1,0:T(8,128)S(1)}, u32[]{:S(2)}) copy-start(f32[2,2,256,256]{2,3,1,0:T(8,128)S(1)} %copy.128) | copy-start | bytes 3145732
  10.1 14.2 %collective-permute-start = (f32[2,2,32,256]{2,3,1,0:T(8,128)}, f32[2,2,32,256]{2,3,1,0:T(8,128)S(1)}, u32[]{:S(2)}, u32[]{:S(2)}) collective-permute-start(f32[2,2,32,256]{2,3,1,0:T(8,128)} %get-tuple-element.96), channel_id=1, source_target_pairs={{0,16},{1,17},{2,18},{3,19},{4,20},{5,21},{6,22},{7,23},{8,24},{9,... | collective-permute-start | bytes 393224 | tf_op jit(solution)/shard_map/ppermute | solution.py:24
  12.5 11.7 %collective-permute-start.1 = (f32[2,2,32,256]{2,3,1,0:T(8,128)}, f32[2,2,32,256]{2,3,1,0:T(8,128)S(1)}, u32[]{:S(2)}, u32[]{:S(2)}) collective-permute-start(f32[2,2,32,256]{2,3,1,0:T(8,128)} %get-tuple-element.97), channel_id=1, source_target_pairs={{16,0},{17,1},{18,2},{19,3},{20,4},{21,5},{22,6},{23,7},{24,8},{25... | collective-permute-start | bytes 393224 | tf_op jit(solution)/shard_map/ppermute | solution.py:26
  24.3 9.5 %copy-start.9 = (f32[2,2,32,256]{2,3,1,0:T(8,128)}, f32[2,2,32,256]{2,3,1,0:T(8,128)S(1)}, u32[]{:S(2)}) copy-start(f32[2,2,32,256]{2,3,1,0:T(8,128)S(1)} %collective-permute-done) | copy-start | bytes 393220
  24.3 9.5 %copy-start.10 = (f32[2,2,32,256]{2,3,1,0:T(8,128)}, f32[2,2,32,256]{2,3,1,0:T(8,128)S(1)}, u32[]{:S(2)}) copy-start(f32[2,2,32,256]{2,3,1,0:T(8,128)S(1)} %collective-permute-done.1) | copy-start | bytes 393220
  24.5 9.3 %collective-permute-start.2 = (f32[2,2,320,32]{2,3,1,0:T(8,128)S(1)}, f32[2,2,320,32]{2,3,1,0:T(8,128)S(1)}, u32[]{:S(2)}, u32[]{:S(2)}) collective-permute-start(f32[2,2,320,32]{2,3,1,0:T(8,128)S(1)} %get-tuple-element.84), channel_id=1, source_target_pairs={{0,1},{1,2},{2,3},{3,4},{4,5},{5,6},{6,7},{7,8},{8,9},{9,10},{10,1... | collective-permute-start | bytes 491528 | tf_op jit(solution)/shard_map/ppermute | solution.py:24
  28.7 11.2 %collective-permute-start.3 = (f32[2,2,320,32]{2,3,1,0:T(8,128)S(1)}, f32[2,2,320,32]{2,3,1,0:T(8,128)S(1)}, u32[]{:S(2)}, u32[]{:S(2)}) collective-permute-start(f32[2,2,320,32]{2,3,1,0:T(8,128)S(1)} %get-tuple-element.85), channel_id=1, source_target_pairs={{1,0},{2,1},{3,2},{4,3},{5,4},{6,5},{7,6},{8,7},{9,8},{10,9},{11,1... | collective-permute-start | bytes 491528 | tf_op jit(solution)/shard_map/ppermute | solution.py:26
  41.8 1.3 copy-start
  45.4 1.9 copy-start.1
  47.3 1.3 copy-start
  50.9 1.9 copy-start.1
  53.1 6.6 %copy-start.6 = (f32[256,256]{0,1:T(8,128)S(1)}, f32[256,256]{0,1:T(8,128)}, u32[]{:S(2)}) copy-start(f32[256,256]{0,1:T(8,128)} %copy.64) | copy-start | bytes 786436
  53.1 6.6 %copy-start.7 = (f32[256,256]{0,1:T(8,128)S(1)}, f32[256,256]{0,1:T(8,128)}, u32[]{:S(2)}) copy-start(f32[256,256]{0,1:T(8,128)} %copy.71) | copy-start | bytes 786436
  53.1 6.6 %copy-start.8 = (f32[2,2,2,256,256]{3,4,0,2,1:T(8,128)S(1)}, f32[2,2,2,256,256]{3,4,0,2,1:T(8,128)}, u32[]{:S(2)}) copy-start(f32[2,2,2,256,256]{3,4,0,2,1:T(8,128)} %get-tuple-element.57) | copy-start | bytes 6291460
  95.9 5.5 %copy-start.4 = (f32[1,1,2,256,256]{3,4,2,1,0:T(8,128)S(1)}, f32[1,1,2,256,256]{3,4,2,1,0:T(8,128)}, u32[]{:S(2)}) copy-start(f32[1,1,2,256,256]{3,4,2,1,0:T(8,128)} %copy.98) | copy-start | bytes 1572868
  148.6 1.3 copy-start.5
  180.4 5.0 %copy-start.13 = (f32[256,256]{0,1:T(8,128)S(1)}, f32[256,256]{0,1:T(8,128)}, u32[]{:S(2)}) copy-start(f32[256,256]{0,1:T(8,128)} %get-tuple-element.66) | copy-start | bytes 786436
  180.4 5.0 %copy-start.14 = (f32[256,256]{0,1:T(8,128)S(1)}, f32[256,256]{0,1:T(8,128)}, u32[]{:S(2)}) copy-start(f32[256,256]{0,1:T(8,128)} %get-tuple-element.67) | copy-start | bytes 786436
  180.4 11.1 %collective-permute-start.4 = (f32[2,2,32,320]{3,2,1,0:T(8,128)S(1)}, f32[2,2,32,320]{3,2,1,0:T(8,128)}, u32[]{:S(2)}, u32[]{:S(2)}) collective-permute-start(f32[2,2,32,320]{3,2,1,0:T(8,128)S(1)} %copy.124), channel_id=1, source_target_pairs={{16,0},{17,1},{18,2},{19,3},{20,4},{21,5},{22,6},{23,7},{24,8},{25... | collective-permute-start | bytes 491528 | tf_op jit(solution)/shard_map/ppermute | solution.py:13
  187.1 9.4 %collective-permute-start.5 = (f32[2,2,32,320]{3,2,1,0:T(8,128)}, f32[2,2,32,320]{3,2,1,0:T(8,128)}, u32[]{:S(2)}, u32[]{:S(2)}) collective-permute-start(f32[2,2,32,320]{3,2,1,0:T(8,128)} %copy.126), channel_id=1, source_target_pairs={{0,16},{1,17},{2,18},{3,19},{4,20},{5,21},{6,22},{7,23},{8,24},{9,... | collective-permute-start | bytes 491528 | tf_op jit(solution)/shard_map/ppermute | solution.py:13
  198.8 118.5 %copy-start.11 = (f32[2,256,256]{1,2,0:T(8,128)S(1)}, f32[2,256,256]{1,2,0:T(8,128)}, u32[]{:S(2)}) copy-start(f32[2,256,256]{1,2,0:T(8,128)} %copy.129) | copy-start | bytes 1572868
  205.5 113.0 %collective-permute-start.6 = (f32[2,2,32,256]{3,2,1,0:T(8,128)}, f32[2,2,32,256]{3,2,1,0:T(8,128)S(1)}, u32[]{:S(2)}, u32[]{:S(2)}) collective-permute-start(f32[2,2,32,256]{3,2,1,0:T(8,128)} %get-tuple-element.91), channel_id=1, source_target_pairs={{1,0},{2,1},{3,2},{4,3},{5,4},{6,5},{7,6},{8,7},{9,8},{10,9},{11,1... | collective-permute-start | bytes 393224 | tf_op jit(solution)/shard_map/ppermute | solution.py:13
  206.8 154.7 %copy-start.3 = (f32[2,2,256,256]{2,3,1,0:T(8,128)S(1)}, f32[2,2,256,256]{2,3,1,0:T(8,128)}, u32[]{:S(2)}) copy-start(f32[2,2,256,256]{2,3,1,0:T(8,128)} %copy-done.2) | copy-start | bytes 3145732
  206.8 112.6 %collective-permute-start.7 = (f32[2,2,32,256]{3,2,1,0:T(8,128)S(1)}, f32[2,2,32,256]{3,2,1,0:T(8,128)S(1)}, u32[]{:S(2)}, u32[]{:S(2)}) collective-permute-start(f32[2,2,32,256]{3,2,1,0:T(8,128)S(1)} %get-tuple-element.90), channel_id=1, source_target_pairs={{0,1},{1,2},{2,3},{3,4},{4,5},{5,6},{6,7},{7,8},{8,9},{9,10},{10,1... | collective-permute-start | bytes 393224 | tf_op jit(solution)/shard_map/ppermute | solution.py:13
Sparse Core Ops, SparseCore 0:
  186.3 130.9 all-reduce.1
where the time goes:
time: 377 us; the launch traced here: 372 us
  waiting for transfers between devices  116 us (31%)
  matrix products  94.9 us (25%)
  local copies, waits for them, and re-layouts  67.2 us (18%)
  blocking collectives  39.5 us (10%)
  starting transfers between devices  21 us (6%)
  between operations  20.6 us (5%)
  other arithmetic  12.9 us (3%)
    psum x1, waiting for transfers between devices, local(): probe_total = lax.psum(probe_grad, ('row', 'col'))  106 us
    pmax x1, blocking collectives, local(): largest = lax.pmax(local_peak, ('row', 'col'))  39.5 us
    dynamic_update_slice x2, local copies, waits for them, and re-layouts, tile_gradient(): lax.dynamic_update_slice(gradient, current + pieces[position], start_at)  27.5 us
    dot_general x6, matrix products, transform(): ic = jnp.einsum('byx,xk->byk', imag_part, cosine, precision=high)  13.1 us
    dot_general x6, matrix products, transform(): rc = jnp.einsum('byx,xk->byk', real_part, cosine, precision=high)  12.6 us
    dot_general x6, matrix products, transform(): jnp.einsum('ky,byx->bkx', sine_tab, mid_im, precision=high)  12.4 us
    dot_general x6, matrix products, transform(): rs = jnp.einsum('byx,xk->byk', real_part, sine_tab, precision=high)  11.8 us
    ppermute x4, starting transfers between devices, passed_along(): lax.ppermute(value, axis, [(source, source + steps) for source in range(i...  11.8 us
  transfers between devices with their start and end apart: 9, of which 3 were waited for; matrix products, arithmetic and copies ran while one was open for 7% of the time, Pallas kernels for 0%

commit v1 on v0

--- a/solution.py
+++ b/solution.py
@@ -151,7 +151,7 @@
     current = object_in
     window = extended(current, (("row", 2), ("col", 3)), RIM)
     gradient, probe_grad = tile_gradient(window, probe_in, offsets, measured, constants)
-    probe_total = lax.psum(probe_grad, ("row", "col"))
+    probe_total = jnp.sum(lax.all_gather(probe_grad, ("row", "col")), 0)
     probe_next = probe_in - probe_rate * probe_total
     descent = rows_then_cols(gradient)
     local_peak = jnp.max(descent[:, 0] ** 2 + descent[:, 1] ** 2)

time: 377 us -> 289 us (0.77)
  waiting for transfers between devices: 116 us -> 15.3 us
  blocking collectives: 39.5 us -> 46.8 us
  other arithmetic: 12.9 us -> 18.7 us
  local copies, waits for them, and re-layouts: 67.2 us -> 63.2 us
    psum x1 -> x0, waiting for transfers between devices: 106 us -> none  [local(): probe_total = lax.psum(probe_grad, ('row', 'col'))]
    ppermute x4, waiting for transfers between devices: 0.01 us -> 7.55 us  [passed_along(): lax.ppermute(value, axis, [(source, source + steps) for source in range(i...]
    pmax x1, blocking collectives: 39.5 us -> 46.8 us  [local(): largest = lax.pmax(local_peak, ('row', 'col'))]
    reduce_sum x0 -> x1, other arithmetic: none -> 6.95 us  [local(): probe_total = jnp.sum(lax.all_gather(probe_grad, ('row', 'col')), 0)]
    unnamed x33 -> x27, local copies, waits for them, and re-layouts: 9.49 us -> 5.24 us
  transfers between devices with their start and end apart: 9 -> 9, of which waited for: 3 -> 4; matrix products, arithmetic and copies ran while one was open for 7% -> 20% of each run, Pallas kernels for 0% -> 0%
where the time goes in v1:
time: 289 us; the launch traced here: 284 us
  matrix products  95 us (33%)
  local copies, waits for them, and re-layouts  63.2 us (22%)
  blocking collectives  46.8 us (16%)
  starting transfers between devices  23.5 us (8%)
  between operations  20.8 us (7%)
  other arithmetic  18.7 us (6%)
  waiting for transfers between devices  15.3 us (5%)
    pmax x1, blocking collectives, local(): largest = lax.pmax(local_peak, ('row', 'col'))  46.8 us
    dynamic_update_slice x2, local copies, waits for them, and re-layouts, tile_gradient(): lax.dynamic_update_slice(gradient, current + pieces[position], start_at)  27.5 us
    dot_general x6, matrix products, transform(): rc = jnp.einsum('byx,xk->byk', real_part, cosine, precision=high)  13.1 us
    dot_general x6, matrix products, transform(): jnp.einsum('ky,byx->bkx', sine_tab, mid_im, precision=high)  12.9 us
    dot_general x6, matrix products, transform(): ic = jnp.einsum('byx,xk->byk', imag_part, cosine, precision=high)  12.6 us
    ppermute x4, starting transfers between devices, passed_along(): lax.ppermute(value, axis, [(source, source + steps) for source in range(i...  12.2 us
    dot_general x6, matrix products, transform(): isn = jnp.einsum('byx,xk->byk', imag_part, sine_tab, precision=high)  11.9 us
    dot_general x6, matrix products, transform(): rs = jnp.einsum('byx,xk->byk', real_part, sine_tab, precision=high)  11.5 us
  transfers between devices with their start and end apart: 9, of which 4 were waited for; matrix products, arithmetic and copies ran while one was open for 20% of the time, Pallas kernels for 0%

profile of v1, /device:TPU:0, one launch (start us, length us, event | category | flops | bytes accessed | tf_op | source)
XLA Modules:
  0.0 283.7 jit_solution(6781548442091855451)
XLA Ops:
  11.5 3.1 %collective-permute-start = (f32[2,2,32,256]{2,3,1,0:T(8,128)}, f32[2,2,32,256]{2,3,1,0:T(8,128)S(1)}, u32[]{:S(2)}, u32[]{:S(2)}) collective-permute-start(f32[2,2,32,256]{2,3,1,0:T(8,128)} %get-tuple-element.96), channel_id=1, source_target_pairs={{0,16},{1,17},{2,18},{3,19},{4,20},{5,21},{6,22},{7,23},{8,24},{9,... | collective-permute-start | bytes 393224 | tf_op jit(solution)/shard_map/ppermute | solution.py:24
  17.4 2.0 copy.98
  21.1 5.5 %collective-permute-start.2 = (f32[2,2,320,32]{2,3,1,0:T(8,128)S(1)}, f32[2,2,320,32]{2,3,1,0:T(8,128)S(1)}, u32[]{:S(2)}, u32[]{:S(2)}) collective-permute-start(f32[2,2,320,32]{2,3,1,0:T(8,128)S(1)} %get-tuple-element.84), channel_id=1, source_target_pairs={{0,1},{1,2},{2,3},{3,4},{4,5},{5,6},{6,7},{7,8},{8,9},{9,10},{10,1... | collective-permute-start | bytes 491528 | tf_op jit(solution)/shard_map/ppermute | solution.py:24
  26.7 2.4 collective-permute-done.3
  29.1 5.3 %collective-permute-done.2 = f32[2,2,320,32]{2,3,1,0:T(8,128)S(1)} collective-permute-done((f32[2,2,320,32]{2,3,1,0:T(8,128)S(1)}, f32[2,2,320,32]{2,3,1,0:T(8,128)S(1)}, u32[]{:S(2)}, u32[]{:S(2)}) %collective-permute-start.2) | collective-permute-done | bytes 163872 | tf_op jit(solution)/shard_map/ppermute | solution.py:24
  36.2 11.3 %while.5 = (s32[]{:T(128)}, f32[2,2,320,320]{2,3,1,0:T(8,128)S(1)}, s32[2,4]{1,0:T(2,128)S(1)}, f32[2,2,2,256,256]{3,4,0,2,1:T(8,128)}, s32[]{:T(128)}) while((s32[]{:T(128)}, f32[2,2,320,320]{2,3,1,0:T(8,128)S(1)}, s32[2,4]{1,0:T(2,128)S(1)}, f32[2,2,2,256,256]{3,4,0,2,1:T(8,128)}, s32[]{:T(128)}) %tuple.63), condition=%wide.while_cond.4, body=%wide.while_body.4.sunk | while | flops 2 | bytes 21495996 | solution.py:91
  47.6 3.4 %fusion.116 = f32[2,256,256]{2,1,0:T(8,128)S(1)} fusion(f32[2,2,2,256,256]{3,4,0,2,1:T(8,128)} %get-tuple-element.57, f32[256,256]{0,1:T(8,128)} %copy.71, f32[256,256]{0,1:T(8,128)} %copy.64), kind=kOutput, calls=%fused_computation.184 | convolution fusion | flops 404029440 | bytes 2097152 | tf_op jit(solution)/shard_map/byx,xk->byk/dot_general | solution.py:54
  50.9 3.2 %fusion.112 = f32[2,256,256]{2,1,0:T(8,128)S(1)} fusion(f32[2,2,2,256,256]{3,4,0,2,1:T(8,128)} %get-tuple-element.57, f32[256,256]{0,1:T(8,128)} %copy.71, f32[256,256]{0,1:T(8,128)} %copy.64), kind=kOutput, calls=%fused_computation.180 | convolution fusion | flops 404029440 | bytes 2097152 | tf_op jit(solution)/shard_map/byx,xk->byk/dot_general | solution.py:56
  61.6 2.3 fusion.23
  73.3 2.1 fusion.21
  84.5 2.1 convolution_subtract_fusion.3
  97.7 2.3 fusion.92
  100.0 1.9 fusion.12
  103.8 1.9 fusion.13
  109.5 2.2 add_bitcast_fusion
  120.9 2.1 fusion.78
  134.1 2.3 fusion.5
  140.1 2.9 %fusion.38 = (f32[256,256]{0,1:T(8,128)S(1)}, f32[256,256]{0,1:T(8,128)S(1)}, f32[2,1,256,256]{2,3,0,1:T(8,128)S(1)}, f32[2,1,256,256]{2,3,0,1:T(8,128)}) fusion(f32[2,256,256]{1,2,0:T(8,128)S(1)} %fusion.1, f32[2,2,2,256,256]{3,4,0,2,1:T(8,128)S(1)} %copy-done.8, f32[256,256]{0,1:T(8,128)S(1)} %copy-done.6, f32[256,256]{0,1:T(8,128)S(1)} %copy-done.7, ...), kind=kOutput, calls=%fused_computation.86 | convolution fusion | flops 405602304 | bytes 4718592 | tf_op jit(solution)/shard_map/ky,byx->bkx/dot_general | solution.py:60
  152.5 13.5 %dynamic_update_slice.6 = f32[2,2,320,320]{2,3,1,0:T(8,128)S(1)} dynamic-update-slice(f32[2,2,320,320]{2,3,1,0:T(8,128)S(1)} %broadcast_in_dim.2, f32[2,2,256,256]{2,3,1,0:T(8,128)} %fusion.25, s32[]{:T(128)} %constant.162.clone.1, s32[]{:T(128)} %constant.162.clone.1, s32[]{:T(128)S(6)} %select_n.155, s32[]{:T(128)S(6)} %select_n.156) | dynamic-update-slice | bytes 2097156 | tf_op jit(solution)/shard_map/dynamic_update_slice | solution.py:120
  165.9 2.4 fusion.27
  168.3 14.0 %dynamic_update_slice.7 = f32[2,2,320,320]{2,3,1,0:T(8,128)S(1)} dynamic-update-slice(f32[2,2,320,320]{2,3,1,0:T(8,128)S(1)} %dynamic_update_slice.6, f32[2,2,256,256]{2,3,1,0:T(8,128)} %fusion.27, s32[]{:T(128)} %constant.162.clone.1, s32[]{:T(128)} %constant.162.clone.1, s32[]{:T(128)S(6)} %select_n.157, s32[]{:T(128)S(6)} %select_n.158) | dynamic-update-slice | bytes 2097156 | tf_op jit(solution)/shard_map/dynamic_update_slice | solution.py:120
  186.1 2.0 copy.126
  188.1 4.4 %collective-permute-start.5 = (f32[2,2,32,320]{3,2,1,0:T(8,128)}, f32[2,2,32,320]{3,2,1,0:T(8,128)}, u32[]{:S(2)}, u32[]{:S(2)}) collective-permute-start(f32[2,2,32,320]{3,2,1,0:T(8,128)} %copy.126), channel_id=1, source_target_pairs={{0,16},{1,17},{2,18},{3,19},{4,20},{5,21},{6,22},{7,23},{8,24},{9,... | collective-permute-start | bytes 491528 | tf_op jit(solution)/shard_map/ppermute | solution.py:13
  192.5 2.0 copy.125
  194.5 2.0 slice_add_fusion.1
  196.6 4.3 %scatter-add.14 = f32[2,2,256,320]{2,3,1,0:T(8,128)S(1)} dynamic-update-slice(f32[2,2,256,320]{2,3,1,0:T(8,128)S(1)} %slice.249, f32[2,2,32,320]{2,3,1,0:T(8,128)} %slice_add_fusion.1, s32[]{:T(128)} %constant.162.clone.1, s32[]{:T(128)} %constant.162.clone.1, s32[]{:T(128)} %constant.175.clone.1, s32[]{:T(128)} %constant.162.clone.1) | dynamic-update-slice | bytes 327684 | tf_op jit(solution)/shard_map/scatter-add | solution.py:134
  202.1 2.7 scatter-add.15
  206.4 5.1 %collective-permute-start.7 = (f32[2,2,32,256]{3,2,1,0:T(8,128)S(1)}, f32[2,2,32,256]{3,2,1,0:T(8,128)S(1)}, u32[]{:S(2)}, u32[]{:S(2)}) collective-permute-start(f32[2,2,32,256]{3,2,1,0:T(8,128)S(1)} %get-tuple-element.90), channel_id=1, source_target_pairs={{0,1},{1,2},{2,3},{3,4},{4,5},{5,6},{6,7},{7,8},{8,9},{9,10},{10,1... | collective-permute-start | bytes 393224 | tf_op jit(solution)/shard_map/ppermute | solution.py:13
  211.5 5.1 %collective-permute-done.6 = f32[2,2,32,256]{3,2,1,0:T(8,128)S(1)} collective-permute-done((f32[2,2,32,256]{3,2,1,0:T(8,128)S(1)}, f32[2,2,32,256]{3,2,1,0:T(8,128)S(1)}, u32[]{:S(2)}, u32[]{:S(2)}) %collective-permute-start.6) | collective-permute-done | bytes 131104 | tf_op jit(solution)/shard_map/ppermute | solution.py:13
  216.7 2.4 collective-permute-done.7
  219.9 46.8 %pmax.7 = f32[]{:T(128)} all-reduce(f32[]{:T(128)} %fusion.29), channel_id=1, replica_groups=mesh['row'=2,'col'=16] {'row','col'}, use_global_device_ids=true, to_apply=%region_1.2 | all-reduce | flops 1 | bytes 8 | tf_op jit(solution)/shard_map/pmax | solution.py:158
  268.9 6.9 %reduce_sum.29 = f32[2,256,256]{2,1,0:T(8,128)S(1)} reduce(f32[32,2,256,256]{3,2,1,0:T(8,128)} %bitcast.294, f32[]{:T(128)} %constant.160.clone.1), dimensions={0}, to_apply=%region_4.5 | reduce | flops 4063232 | bytes 17301508 | tf_op jit(solution)/shard_map/reduce_sum | solution.py:154
  (124 shorter events, 101.7 us)
Async XLA Ops:
  7.2 7.5 %copy-start.11 = (f32[2,256,256]{2,1,0:T(8,128)S(1)}, f32[2,256,256]{2,1,0:T(8,128)}, u32[]{:S(2)}) copy-start(f32[2,256,256]{2,1,0:T(8,128)} %param.13) | copy-start | bytes 1572868
  7.2 261.7 %all-gather.3.cloned.1.call-start = ((), (), s32[]{:S(2)}) async-start(), calls=%async_computation | async-start | bytes 17301504 | tf_op jit(solution)/shard_map/all_gather | solution.py:154
  8.8 25.6 %copy-start.2 = (f32[2,2,256,256]{2,3,1,0:T(8,128)}, f32[2,2,256,256]{2,3,1,0:T(8,128)S(1)}, u32[]{:S(2)}) copy-start(f32[2,2,256,256]{2,3,1,0:T(8,128)S(1)} %copy.128) | copy-start | bytes 3145732
  10.1 9.4 %copy-start.13 = (s32[1,1,2,2]{3,2,1,0:T(2,128)S(1)}, s32[1,1,2,2]{3,2,1,0:T(2,128)}, u32[]{:S(2)}) copy-start(s32[1,1,2,2]{3,2,1,0:T(2,128)} %param.14) | copy-start | bytes 52
  10.1 9.5 %collective-permute-start.1 = (f32[2,2,32,256]{2,3,1,0:T(8,128)}, f32[2,2,32,256]{2,3,1,0:T(8,128)S(1)}, u32[]{:S(2)}, u32[]{:S(2)}) collective-permute-start(f32[2,2,32,256]{2,3,1,0:T(8,128)} %get-tuple-element.97), channel_id=1, source_target_pairs={{16,0},{17,1},{18,2},{19,3},{20,4},{21,5},{22,6},{23,7},{24,8},{25... | collective-permute-start | bytes 393224 | tf_op jit(solution)/shard_map/ppermute | solution.py:26
  11.5 8.0 %collective-permute-start = (f32[2,2,32,256]{2,3,1,0:T(8,128)}, f32[2,2,32,256]{2,3,1,0:T(8,128)S(1)}, u32[]{:S(2)}, u32[]{:S(2)}) collective-permute-start(f32[2,2,32,256]{2,3,1,0:T(8,128)} %get-tuple-element.96), channel_id=1, source_target_pairs={{0,16},{1,17},{2,18},{3,19},{4,20},{5,21},{6,22},{7,23},{8,24},{9,... | collective-permute-start | bytes 393224 | tf_op jit(solution)/shard_map/ppermute | solution.py:24
  19.5 9.5 %copy-start.9 = (f32[2,2,32,256]{2,3,1,0:T(8,128)}, f32[2,2,32,256]{2,3,1,0:T(8,128)S(1)}, u32[]{:S(2)}) copy-start(f32[2,2,32,256]{2,3,1,0:T(8,128)S(1)} %collective-permute-done.1) | copy-start | bytes 393220
  19.6 9.5 %copy-start.10 = (f32[2,2,32,256]{2,3,1,0:T(8,128)}, f32[2,2,32,256]{2,3,1,0:T(8,128)S(1)}, u32[]{:S(2)}) copy-start(f32[2,2,32,256]{2,3,1,0:T(8,128)S(1)} %collective-permute-done) | copy-start | bytes 393220
  19.8 9.3 %collective-permute-start.3 = (f32[2,2,320,32]{2,3,1,0:T(8,128)S(1)}, f32[2,2,320,32]{2,3,1,0:T(8,128)S(1)}, u32[]{:S(2)}, u32[]{:S(2)}) collective-permute-start(f32[2,2,320,32]{2,3,1,0:T(8,128)S(1)} %get-tuple-element.85), channel_id=1, source_target_pairs={{1,0},{2,1},{3,2},{4,3},{5,4},{6,5},{7,6},{8,7},{9,8},{10,9},{11,1... | collective-permute-start | bytes 491528 | tf_op jit(solution)/shard_map/ppermute | solution.py:26
  21.1 13.3 %collective-permute-start.2 = (f32[2,2,320,32]{2,3,1,0:T(8,128)S(1)}, f32[2,2,320,32]{2,3,1,0:T(8,128)S(1)}, u32[]{:S(2)}, u32[]{:S(2)}) collective-permute-start(f32[2,2,320,32]{2,3,1,0:T(8,128)S(1)} %get-tuple-element.84), channel_id=1, source_target_pairs={{0,1},{1,2},{2,3},{3,4},{4,5},{5,6},{6,7},{7,8},{8,9},{9,10},{10,1... | collective-permute-start | bytes 491528 | tf_op jit(solution)/shard_map/ppermute | solution.py:24
  36.2 1.3 copy-start
  39.8 1.9 copy-start.1
  41.7 1.3 copy-start
  45.3 1.9 copy-start.1
  47.5 6.6 %copy-start.6 = (f32[256,256]{0,1:T(8,128)S(1)}, f32[256,256]{0,1:T(8,128)}, u32[]{:S(2)}) copy-start(f32[256,256]{0,1:T(8,128)} %copy.71) | copy-start | bytes 786436
  47.6 6.6 %copy-start.7 = (f32[256,256]{0,1:T(8,128)S(1)}, f32[256,256]{0,1:T(8,128)}, u32[]{:S(2)}) copy-start(f32[256,256]{0,1:T(8,128)} %copy.64) | copy-start | bytes 786436
  47.6 6.6 %copy-start.8 = (f32[2,2,2,256,256]{3,4,0,2,1:T(8,128)S(1)}, f32[2,2,2,256,256]{3,4,0,2,1:T(8,128)}, u32[]{:S(2)}) copy-start(f32[2,2,2,256,256]{3,4,0,2,1:T(8,128)} %get-tuple-element.57) | copy-start | bytes 6291460
  90.3 5.5 %copy-start.4 = (f32[1,1,2,256,256]{3,4,2,1,0:T(8,128)S(1)}, f32[1,1,2,256,256]{3,4,2,1,0:T(8,128)}, u32[]{:S(2)}) copy-start(f32[1,1,2,256,256]{3,4,2,1,0:T(8,128)} %copy.98) | copy-start | bytes 1572868
  151.0 1.3 copy-start.5
  184.4 8.1 %collective-permute-start.4 = (f32[2,2,32,320]{3,2,1,0:T(8,128)}, f32[2,2,32,320]{3,2,1,0:T(8,128)}, u32[]{:S(2)}, u32[]{:S(2)}) collective-permute-start(f32[2,2,32,320]{3,2,1,0:T(8,128)} %copy.124), channel_id=1, source_target_pairs={{16,0},{17,1},{18,2},{19,3},{20,4},{21,5},{22,6},{23,7},{24,8},{25... | collective-permute-start | bytes 491528 | tf_op jit(solution)/shard_map/ppermute | solution.py:13
  188.1 12.8 %collective-permute-start.5 = (f32[2,2,32,320]{3,2,1,0:T(8,128)}, f32[2,2,32,320]{3,2,1,0:T(8,128)}, u32[]{:S(2)}, u32[]{:S(2)}) collective-permute-start(f32[2,2,32,320]{3,2,1,0:T(8,128)} %copy.126), channel_id=1, source_target_pairs={{0,16},{1,17},{2,18},{3,19},{4,20},{5,21},{6,22},{7,23},{8,24},{9,... | collective-permute-start | bytes 491528 | tf_op jit(solution)/shard_map/ppermute | solution.py:13
  204.9 62.5 %copy-start.3 = (f32[2,2,256,256]{2,3,1,0:T(8,128)S(1)}, f32[2,2,256,256]{2,3,1,0:T(8,128)}, u32[]{:S(2)}) copy-start(f32[2,2,256,256]{2,3,1,0:T(8,128)} %copy-done.2) | copy-start | bytes 3145732
  204.9 11.8 %collective-permute-start.6 = (f32[2,2,32,256]{3,2,1,0:T(8,128)S(1)}, f32[2,2,32,256]{3,2,1,0:T(8,128)S(1)}, u32[]{:S(2)}, u32[]{:S(2)}) collective-permute-start(f32[2,2,32,256]{3,2,1,0:T(8,128)S(1)} %get-tuple-element.91), channel_id=1, source_target_pairs={{1,0},{2,1},{3,2},{4,3},{5,4},{6,5},{7,6},{8,7},{9,8},{10,9},{11,1... | collective-permute-start | bytes 393224 | tf_op jit(solution)/shard_map/ppermute | solution.py:13
  206.4 12.7 %collective-permute-start.7 = (f32[2,2,32,256]{3,2,1,0:T(8,128)S(1)}, f32[2,2,32,256]{3,2,1,0:T(8,128)S(1)}, u32[]{:S(2)}, u32[]{:S(2)}) collective-permute-start(f32[2,2,32,256]{3,2,1,0:T(8,128)S(1)} %get-tuple-element.90), channel_id=1, source_target_pairs={{0,1},{1,2},{2,3},{3,4},{4,5},{5,6},{6,7},{7,8},{8,9},{9,10},{10,1... | collective-permute-start | bytes 393224 | tf_op jit(solution)/shard_map/ppermute | solution.py:13
  268.9 7.0 %copy-start.12 = (f32[2,256,256]{2,1,0:T(8,128)S(1)}, f32[2,256,256]{2,1,0:T(8,128)}, u32[]{:S(2)}) copy-start(f32[2,256,256]{2,1,0:T(8,128)} %param.13) | copy-start | bytes 1572868
Sparse Core Ops, SparseCore 0:
  144.2 121.6 all-gather.2
